TPU v7x, 16 devices: a whole 2x2x2 slice. The times are simulated.
16 devices in a mesh: col: 2 (over z), row: 8 (over y, x, core).
Axes of the slice: x: 2, y: 2, z: 2, core: 2. Of those that a mesh axis runs over, the one named last changes fastest.
Arguments:
- t_amp: float32 [576, 10816], P('row', 'col')
- d_denom: float32 [576, 10816], P('row', 'col')
- v_oovv: bfloat16 [576, 10816], P('row', 'col')
- v_vvvv: bfloat16 [10816, 10816], P('row', 'col')
- v_oooo: bfloat16 [576, 576], replicated
- w_ovov: bfloat16 [2496, 2496], P(None, 'col')
Outputs:
- output: float32 [2496, 2496], P('row', 'col')
All inputs are finite; a program needn't handle non-finite values.
Results may differ from a plain program's by a relative error of at most 0.001.
Values are sent between devices in bfloat16 or wider.
A program may use at most 1 GiB of HBM per device.

v0:
```python
import math
import jax
import jax.numpy as jnp
from jax import lax
from jax.sharding import PartitionSpec as P


def solution(mesh):
    row_n = mesh.shape["row"]
    col_n = mesh.shape["col"]

    def local_sweep(t_blk, d_blk, voovv_blk, vvvvv_blk, oooo_blk, wr_blk):
        n_occ = math.isqrt(oooo_blk.shape[0])
        n_vir = wr_blk.shape[0] // n_occ
        occ_r = n_occ // row_n
        occ_c = n_occ // col_n
        vir_c = n_vir // col_n
        t_bf = t_blk.astype(jnp.bfloat16)
        t_rows = lax.all_gather(t_bf, "col", axis=1, tiled=True)
        t_ladder = lax.all_to_all(t_rows, "row", 1, 0, tiled=True)
        ladder_part = jnp.dot(t_ladder, vvvvv_blk, preferred_element_type=jnp.float32)
        r_ladder = lax.psum_scatter(ladder_part, "row", scatter_dimension=0, tiled=True)
        t_cols = lax.all_gather(t_bf, "row", axis=0, tiled=True)
        x_part = lax.dot_general(voovv_blk, t_cols, (((1,), (1,)), ((), ())), preferred_element_type=jnp.float32)
        x_rows = lax.psum(x_part, "col")
        x_cols = lax.all_to_all(x_rows, "row", 1, 0, tiled=True)
        w_hole = (oooo_blk.astype(jnp.float32) + 0.5 * x_cols).astype(jnp.bfloat16)
        r_hole = lax.dot_general(w_hole, t_cols, (((0,), (0,)), ((), ())), preferred_element_type=jnp.float32)
        amp_four = t_rows.reshape(occ_r, n_occ, n_vir, n_vir)
        wr_three = wr_blk.reshape(n_occ, n_vir, occ_c * n_vir)
        r_mixed = jnp.einsum("ikac,kcn->ian", amp_four, wr_three, preferred_element_type=jnp.float32)
        r_mixed = r_mixed.reshape(occ_r, n_vir, occ_c, n_vir)
        mixed_entry = lax.all_to_all(r_mixed, "col", 1, 2, tiled=True)
        swap_rows = lax.all_to_all(mixed_entry, "row", 2, 0, tiled=True)
        swap_full = lax.all_to_all(swap_rows, "col", 3, 1, tiled=True)
        mixed_image = jnp.transpose(swap_full, (2, 3, 0, 1))
        base_sum = (voovv_blk.astype(jnp.float32) + r_ladder + r_hole).reshape(occ_r, n_occ, vir_c, n_vir)
        d_four = d_blk.reshape(occ_r, n_occ, vir_c, n_vir)
        total_sum = (jnp.transpose(base_sum, (0, 2, 1, 3)) + mixed_entry + mixed_image) / jnp.transpose(d_four, (0, 2, 1, 3))
        t_pairs = lax.all_to_all(total_sum, "col", 2, 1, tiled=True)
        return t_pairs.reshape(occ_r * n_vir, occ_c * n_vir)

    return jax.shard_map(
        local_sweep,
        mesh=mesh,
        in_specs=(P("row", "col"), P("row", "col"), P("row", "col"), P("row", "col"), P(None, "row"), P(None, "col")),
        out_specs=P("row", "col"),
        check_vma=False,
    )
```

profile of v0, /device:TPU:0, one launch (start us, length us, event | category | flops | bytes accessed | tf_op | source)
XLA Modules:
  0.0 332.3 jit_solution(5577297527242415468)
XLA Ops:
  6.5 0.0 copy-start.1
  6.5 0.0 all-gather.6.cloned.1.call-start
  6.5 2.5 convert_bitcast_fusion
  9.0 0.0 all-gather.6.cloned.1.call-update
  9.1 0.0 all-gather.4.cloned.1.call-start
  9.1 0.0 copy-done.1
  9.1 1.0 convert_element_type.13
  10.1 0.0 all-gather.4.cloned.1.call-update
  10.1 27.1 %all-gather.6.cloned.1.call-done = bf16[2,5408,72]{1,2,0:T(8,128)(2,1)} async-done(((bf16[1,5408,72]{1,2,0:T(8,128)(2,1)}), bf16[2,5408,72]{1,2,0:T(8,128)(2,1)}) %all-gather.6.cloned.1.call-update) | async-done | bytes 1557520 | tf_op jit(solution)/shard_map/all_gather | solution.py:19
  37.2 2.6 copy.48
  39.9 1.2 reshape.42
  41.1 2.3 all_to_all.74
  43.3 1.4 copy.49
  44.7 0.0 copy-start.2
  44.7 4.4 %all-to-all-start = ((bf16[72,8,1352]{2,0,1:T(8,128)(2,1)}), bf16[72,8,1352]{2,0,1:T(8,128)(2,1)}, u32[]{:S(2)}, u32[]{:S(2)}) async-start(bf16[72,8,1352]{2,0,1:T(8,128)(2,1)} %copy.49), calls=%async_computation | async-start | bytes 3244032 | tf_op jit(solution)/shard_map/all_to_all | solution.py:20
  49.1 0.0 all-reduce.3.cloned.1.call-start
  49.2 46.0 %all-gather.4.cloned.1.call-done = bf16[576,5408]{1,0:T(8,128)(2,1)} async-done(((bf16[72,5408]{1,0:T(8,128)(2,1)}), bf16[576,5408]{1,0:T(8,128)(2,1)}) %all-gather.4.cloned.1.call-update) | async-done | bytes 6230032 | tf_op jit(solution)/shard_map/all_gather | solution.py:23
  95.2 0.0 copy-done.2
  95.2 4.8 %fusion.11 = f32[72,576]{1,0:T(8,128)S(1)} fusion(bf16[72,5408]{1,0:T(8,128)(2,1)S(1)} %copy-done.2, bf16[576,5408]{1,0:T(8,128)(2,1)} %all-gather.4.cloned.1.call-done), kind=kOutput, calls=%fused_computation.15 | convolution fusion | flops 448561152 | bytes 7174656 | tf_op jit(solution)/shard_map/dot_general | solution.py:24
  100.0 0.2 all_to_all.78
  100.2 0.8 copy.50
  101.0 0.0 all-reduce.3.cloned.1.call-update
  101.0 0.0 reduce-scatter.4.cloned.1.call-start
  101.0 0.0 all-to-all-done
  101.1 16.6 %fusion.10 = f32[576,5408]{1,0:T(8,128)} fusion(bf16[576,1352]{1,0:T(8,128)(2,1)} %bitcast.4, bf16[1352,5408]{1,0:T(8,128)(2,1)} %param.9), kind=kOutput, calls=%fused_computation.14 | convolution fusion | flops 8422981632 | bytes 28640768 | tf_op jit(solution)/shard_map/dot_general | solution.py:21
  117.7 0.0 reduce-scatter.4.cloned.1.call-update
  117.7 10.2 %copy.51 = bf16[1248,104,24]{1,2,0:T(8,128)(2,1)} copy(bf16[1248,104,24]{0,1,2:T(8,128)(2,1)} %bitcast.88) | data formatting | bytes 12460032 | tf_op jit(solution)/shard_map/ikac,kcn->ian/dot_general | solution.py:31
  127.9 3.3 reshape.43
  131.2 6.1 %fusion.4 = f32[3,104,12,104]{3,1,2,0:T(8,128)S(1)} fusion(bf16[12,104,104,24]{2,3,1,0:T(8,128)(2,1)} %bitcast.87, bf16[3,24,104,104,1]{3,2,1,0,4:T(8,128)(2,1)} %reshape.43), kind=kOutput, calls=%fused_computation.10 | convolution fusion | flops 1943764992 | bytes 9345024 | tf_op jit(solution)/shard_map/ikac,kcn->ian/dot_general | solution.py:31
  137.3 0.4 copy.53
  137.7 33.0 %all_to_all.101 = f32[3,104,12,104]{3,2,0,1:T(8,128)S(1)} all-to-all(f32[3,104,12,104]{3,2,0,1:T(8,128)S(1)} %copy.53), channel_id=1, replica_groups=mesh['col'=2,'row'=8] {'col'}, dimensions={1} | all-to-all | bytes 3115008 | tf_op jit(solution)/shard_map/all_to_all | solution.py:33
  170.8 0.6 copy.68
  171.3 34.7 %all_to_all.102 = f32[3,52,24,104]{3,1,0,2:T(8,128)S(1)} all-to-all(f32[3,52,24,104]{3,1,0,2:T(8,128)S(1)} %bitcast.86), channel_id=1, replica_groups=mesh['col'=2,'row'=8] {'row'}, dimensions={2} | all-to-all | bytes 3115008 | tf_op jit(solution)/shard_map/all_to_all | solution.py:34
  206.0 1.4 copy.57
  207.5 4.6 %copy.58 = f32[24,52,3,104]{1,0,2,3:T(8,128)} copy(f32[24,52,3,104]{3,1,2,0:T(8,128)} %bitcast.83) | data formatting | bytes 3115008 | tf_op jit(solution)/shard_map/all_to_all | solution.py:34
  212.1 7.9 %reshape.48 = f32[2,1,194688]{2,1,0:T(1,128)} reshape(f32[104,3,24,52]{3,2,1,0:T(8,128)} %bitcast.76) | data formatting | bytes 3115008
  220.0 0.0 copy-start.3
  220.0 23.4 %all_to_all.103 = f32[2,1,194688]{2,1,0:T(1,128)} all-to-all(f32[2,1,194688]{2,1,0:T(1,128)} %reshape.48), channel_id=1, replica_groups=mesh['col'=2,'row'=8] {'col'}, dimensions={0} | all-to-all | bytes 3115008 | tf_op jit(solution)/shard_map/all_to_all | solution.py:35
  243.4 0.0 all-reduce.3.cloned.1.call-done
  243.4 4.1 %all-to-all-start.1 = ((f32[72,8,72]{2,0,1:T(8,128)}), f32[72,8,72]{2,0,1:T(8,128)}, u32[]{:S(2)}, u32[]{:S(2)}) async-start(f32[72,8,72]{2,0,1:T(8,128)} %all-reduce.3.cloned.1.call-done), calls=%async_computation.1 | async-start | bytes 589824 | tf_op jit(solution)/shard_map/all_to_all | solution.py:26
  247.5 0.0 copy-done.3
  247.5 0.6 dynamic-slice
  248.7 3.3 reshape.31
  252.0 2.0 copy.55
  254.0 0.6 broadcast.5
  254.5 6.3 %reduce = f32[2,194688]{1,0:T(2,128)S(1)} reduce(f32[2,1,194688]{2,1,0:T(1,128)} %all_to_all.103, f32[]{:T(128)} %broadcast.5), dimensions={1}, to_apply=%all_to_all.88.reduce_sub_computation | reduce | bytes 3115012 | tf_op jit(solution)/shard_map/all_to_all | solution.py:35
  260.8 7.7 %reshape.49 = f32[104,3,24,52]{3,2,1,0:T(8,128)} reshape(f32[2,194688]{1,0:T(2,128)S(1)} %reduce) | data formatting | bytes 3115008
  268.5 6.9 %copy.80 = f32[24,52,3,2,52]{1,3,0,4,2:T(2,128)} copy(f32[24,52,3,2,52]{1,0,2,4,3:T(8,128)} %bitcast.77) | data formatting | bytes 3115008 | tf_op jit(solution)/shard_map/all_to_all | solution.py:35
  275.4 5.1 %all_to_all.91 = f32[24,104,3,52]{1,0,3,2:T(8,128)} reshape(f32[24,2,52,3,52]{2,1,0,4,3:T(2,128)} %bitcast.78) | data formatting | bytes 3115008 | tf_op jit(solution)/shard_map/all_to_all | solution.py:35
  280.4 0.0 all-to-all-done.1
  280.4 1.0 broadcast_multiply_fusion
  281.4 1.1 fusion.9
  282.5 0.0 reduce-scatter.4.cloned.1.call-done
  282.5 5.6 %convolution_add_fusion = f32[72,5408]{1,0:T(8,128)} fusion(bf16[576,72]{1,0:T(8,128)(2,1)S(1)} %fusion.9, bf16[576,5408]{1,0:T(8,128)(2,1)} %all-gather.4.cloned.1.call-done, f32[72,5408]{1,0:T(8,128)} %reduce-scatter.4.cloned.1.call-done, bf16[72,5408]{1,0:T(8,128)(2,1)S(1)} %copy-done.2), kind=kOutput, calls=%fused_computation.3 | convolution fusion | flops 449729280 | bytes 10206720 | tf_op jit(solution)/shard_map/dot_general | solution.py:28
  288.1 0.0 copy-start
  288.1 3.4 %reshape.28 = f32[3,24,52,104]{3,2,1,0:T(8,128)} reshape(f32[72,5408]{1,0:T(8,128)} %convolution_add_fusion) | data formatting | bytes 3115008 | tf_op jit(solution)/shard_map/reshape | solution.py:37
  291.6 0.0 copy-done
  291.6 3.5 %bitcast_divide_fusion = f32[3,52,24,104]{3,1,2,0:T(8,128)S(1)} fusion(f32[3,24,52,104]{3,2,1,0:T(8,128)S(1)} %copy-done, f32[3,52,24,104]{3,1,2,0:T(8,128)} %bitcast.82, f32[3,24,52,104]{3,2,1,0:T(8,128)} %reshape.28, f32[24,104,3,52]{1,0,3,2:T(8,128)} %all_to_all.91), kind=kLoop, calls=%fused_computation.6 | loop fusion | flops 1168128 | bytes 7787520 | tf_op jit(solution)/shard_map/div | solution.py:39
  295.1 0.1 copy.62
  295.2 27.8 %all_to_all.104 = f32[3,52,24,104]{3,1,0,2:T(8,128)S(1)} all-to-all(f32[3,52,24,104]{3,1,0,2:T(8,128)S(1)} %copy.62), channel_id=1, replica_groups=mesh['col'=2,'row'=8] {'col'}, dimensions={2} | all-to-all | bytes 3115008 | tf_op jit(solution)/shard_map/all_to_all | solution.py:40
  323.0 0.4 copy.81
  323.4 2.3 reshape.32
Async XLA Ops:
  6.5 2.6 copy-start.1
  6.5 30.7 %all-gather.6.cloned.1.call-start = ((), (), s32[]{:S(2)}) async-start(), calls=%async_computation.9 | async-start | bytes 2377728 | tf_op jit(solution)/shard_map/all_gather | solution.py:19
  9.1 86.2 %all-gather.4.cloned.1.call-start = ((), (), s32[]{:S(2)}) async-start(), calls=%async_computation.7 | async-start | bytes 7133184 | tf_op jit(solution)/shard_map/all_gather | solution.py:23
  44.7 50.5 %copy-start.2 = (bf16[72,5408]{1,0:T(8,128)(2,1)S(1)}, bf16[72,5408]{1,0:T(8,128)(2,1)}, u32[]{:S(2)}) copy-start(bf16[72,5408]{1,0:T(8,128)(2,1)} %param.8) | copy-start | bytes 2336260
  44.7 56.3 %all-to-all-start = ((bf16[72,8,1352]{2,0,1:T(8,128)(2,1)}), bf16[72,8,1352]{2,0,1:T(8,128)(2,1)}, u32[]{:S(2)}, u32[]{:S(2)}) async-start(bf16[72,8,1352]{2,0,1:T(8,128)(2,1)} %copy.49), calls=%async_computation | async-start | bytes 3244032 | tf_op jit(solution)/shard_map/all_to_all | solution.py:20
  49.1 194.3 %all-reduce.3.cloned.1.call-start = ((), (), s32[]{:S(2)}) async-start(), calls=%async_computation.8 | async-start | bytes 589824 | tf_op jit(solution)/shard_map/psum | solution.py:25
  101.0 181.5 %reduce-scatter.4.cloned.1.call-start = ((), (), s32[]{:S(2)}) async-start(), calls=%async_computation.10 | async-start | bytes 14266368
  220.0 27.5 %copy-start.3 = (u32[16]{0:T(128)S(1)}, u32[16]{0:T(128)}, u32[]{:S(2)}) copy-start(u32[16]{0:T(128)} %constant.2) | copy-start | bytes 196
  243.4 37.0 %all-to-all-start.1 = ((f32[72,8,72]{2,0,1:T(8,128)}), f32[72,8,72]{2,0,1:T(8,128)}, u32[]{:S(2)}, u32[]{:S(2)}) async-start(f32[72,8,72]{2,0,1:T(8,128)} %all-reduce.3.cloned.1.call-done), calls=%async_computation.1 | async-start | bytes 589824 | tf_op jit(solution)/shard_map/all_to_all | solution.py:26
  288.1 3.5 %copy-start = (f32[3,24,52,104]{3,2,1,0:T(8,128)S(1)}, f32[3,24,52,104]{3,2,1,0:T(8,128)}, u32[]{:S(2)}) copy-start(f32[3,24,52,104]{3,2,1,0:T(8,128)} %reshape.31) | copy-start | bytes 4672516
Sparse Core Ops, SparseCore 0:
  9.2 27.9 all-gather.5
  39.1 56.1 all-gather.3
  101.1 19.7 all-reduce.2
  124.3 100.6 reduce-scatter.3
where the time goes:
time: 333 us; the launch traced here: 332 us
  blocking collectives  119 us (36%)
  waiting for transfers between devices  73.2 us (22%)
  local copies, waits for them, and re-layouts  69.1 us (21%)
  matrix products  33.1 us (10%)
  other arithmetic  15.3 us (5%)
  between operations  13.9 us (4%)
  starting transfers between devices  8.61 us (3%)
    all_gather x1, waiting for transfers between devices, local_sweep(): t_cols = lax.all_gather(t_bf, 'row', axis=0, tiled=True)  46 us
    all_to_all x1, blocking collectives, local_sweep(): swap_rows = lax.all_to_all(mixed_entry, 'row', 2, 0, tiled=True)  34.7 us
    all_to_all x1, blocking collectives, local_sweep(): mixed_entry = lax.all_to_all(r_mixed, 'col', 1, 2, tiled=True)  33 us
    all_to_all x1, blocking collectives, local_sweep(): t_pairs = lax.all_to_all(total_sum, 'col', 2, 1, tiled=True)  27.8 us
    all_gather x1, waiting for transfers between devices, local_sweep(): t_rows = lax.all_gather(t_bf, 'col', axis=1, tiled=True)  27.1 us
    all_to_all x1, blocking collectives, local_sweep(): swap_full = lax.all_to_all(swap_rows, 'col', 3, 1, tiled=True)  23.4 us
    unnamed x11, local copies, waits for them, and re-layouts  16.7 us
    dot_general x1, matrix products, local_sweep(): jnp.dot(t_ladder, vvvvv_blk, preferred_element_type=jnp.float32)  16.6 us
  transfers between devices with their start and end apart: 6, of which 2 were waited for; matrix products, arithmetic and copies ran while one was open for 28% of the time, Pallas kernels for 0%

commit v1 on v0

v1 whole, which is shorter than its diff:
```python
import functools
import math
import jax
import jax.numpy as jnp
from jax import lax
from jax.experimental import pallas as pl
from jax.experimental.pallas import tpu as pltpu
from jax.sharding import PartitionSpec as P

MESH = pl.DeviceIdType.MESH
CHUNK = 512
HALF = CHUNK // 2


def blk(dk, dy, dx):
    return dk * 4 + dy * 2 + dx


def coords():
    r = lax.axis_index("row")
    c = lax.axis_index("col")
    return r, c, r // 4, (r // 2) % 2, r % 2


def neighbours():
    r, c, y, x, k = coords()
    return {
        "k": {"row": r + 1 - 2 * k},
        "x": {"row": r + 2 * (1 - 2 * x)},
        "y": {"row": r + 4 * (1 - 2 * y)},
        "z": {"col": 1 - c},
    }


def enter(near, extra=()):
    sem = pltpu.get_barrier_semaphore()
    peers = list(near.values()) + list(extra)
    for dev in peers:
        pl.semaphore_signal(sem, inc=1, device_id=dev, device_id_type=MESH)
    pl.semaphore_wait(sem, len(peers))


def rcopy(src, dst, ssem, rsem, dev):
    return pltpu.make_async_remote_copy(
        src_ref=src, dst_ref=dst, send_sem=ssem, recv_sem=rsem, device_id=dev, device_id_type=MESH
    )


def gather_body(p_ref, g_ref, zp_ref, tl_ref, loc_sem, gs, gr, zs, zr, ls, lr):
    r, c, y, x, k = coords()
    near = neighbours()
    diag = {"row": near["x"]["row"] + 1 - 2 * k}
    enter(near, (diag,))
    own = pltpu.make_async_copy(p_ref, g_ref.at[0], loc_sem.at[0])
    own.start()
    bx, by, bd = blk(0, 0, 1), blk(0, 1, 0), blk(0, 1, 1)

    def to_x(q):
        return rcopy(p_ref.at[q], g_ref.at[bx, q], gs.at[bx, q], gr.at[bx, q], near["x"])

    def to_y(q):
        return rcopy(p_ref.at[q], g_ref.at[by, q], gs.at[by, q], gr.at[by, q], near["y"])

    def to_z(q):
        return rcopy(p_ref.at[q], zp_ref.at[q], zs.at[q], zr.at[q], near["z"])

    def to_k(b, q):
        src = p_ref.at[q] if b == 0 else g_ref.at[b, q]
        return rcopy(src, g_ref.at[4 + b, q], gs.at[4 + b, q], gr.at[4 + b, q], near["k"])

    def to_d(q):
        if q < 2:
            return rcopy(g_ref.at[bx, q], g_ref.at[bd, q], gs.at[bd, q], gr.at[bd, q], near["y"])
        return rcopy(g_ref.at[by, q], g_ref.at[bd, q], gs.at[bd, q], gr.at[bd, q], near["x"])

    for s in range(4):
        to_x(s).start()
        to_y((s + 2) % 4).start()
        to_z(s).start()
        to_k(0, s).start()
    for s in range(4):
        to_x(s).wait_recv()
        if s < 2:
            to_d(s).start()
        to_k(bx, s).start()
        q = (s + 2) % 4
        to_y(q).wait_recv()
        if s < 2:
            to_d(q).start()
        to_k(by, q).start()
    for q in range(4):
        to_z(q).wait_recv()
    q_own = 2 * x + k

    def side(dk, dx):
        q = 2 * (x + dx * (1 - 2 * x)) + k + dk * (1 - 2 * k)
        b = blk(dk, 0, dx)
        if dk == 0:
            dev = near["x"]
        else:
            dev = diag if dx else near["k"]
        return rcopy(zp_ref.at[q], tl_ref.at[b], ls.at[b], lr.at[b], dev)

    keep = pltpu.make_async_copy(zp_ref.at[q_own], tl_ref.at[0], loc_sem.at[1])

    @pl.when(y != c)
    def _():
        keep.start()
        for dk, dx in ((0, 1), (1, 1), (1, 0)):
            side(dk, dx).start()

    def up(dk, dx):
        b = blk(dk, 1, dx)
        return rcopy(g_ref.at[b, q_own], tl_ref.at[b], ls.at[b], lr.at[b], near["z"])

    for s in range(4):
        q = (0, 2, 1, 3)[s]
        to_d(q).wait_recv()
        to_k(bd, q).start()
    for q in range(4):
        for b in (by, bx, 0, bd):
            to_k(b, q).wait_recv()

    @pl.when(y == c)
    def _():
        for dk in (0, 1):
            for dx in (0, 1):
                up(dk, dx).start()
        for dk in (0, 1):
            for dx in (0, 1):
                up(dk, dx).wait_send()

    @pl.when(y != c)
    def _():
        keep.wait()
        for dk, dx in ((0, 1), (1, 1), (1, 0)):
            side(dk, dx).wait_send()
            side(dk, dx).wait_recv()
        for dk in (0, 1):
            for dx in (0, 1):
                up(dk, dx).wait_recv()

    own.wait()
    for q in range(4):
        to_x(q).wait_send()
        to_y(q).wait_send()
        to_z(q).wait_send()
        to_d(q).wait_send()
        for b in (0, bx, by, bd):
            to_k(b, q).wait_send()


def gather(p):
    _, rows, cols = p.shape
    dma = pltpu.SemaphoreType.DMA
    any_spec = pl.BlockSpec(memory_space=pl.ANY)
    return pl.pallas_call(
        gather_body,
        name="amp_gather",
        out_shape=(
            jax.ShapeDtypeStruct((8, 4, rows, cols), p.dtype),
            jax.ShapeDtypeStruct((4, rows, cols), p.dtype),
            jax.ShapeDtypeStruct((8, rows, cols), p.dtype),
        ),
        in_specs=[any_spec],
        out_specs=(any_spec, any_spec, any_spec),
        scratch_shapes=[
            dma((2,)), dma((8, 4)), dma((8, 4)), dma((4,)), dma((4,)), dma((8,)), dma((8,)),
        ],
        compiler_params=pltpu.CompilerParams(collective_id=0, has_side_effects=True),
        cost_estimate=pl.CostEstimate(flops=30_000_000_000, bytes_accessed=10_000_000, transcendentals=0),
    )(p)


def ladder_body(n_chunk, lag2, lag3, tl_ref, wt_ref, im_ref, v_ref, t_ref, out_ref,
                sd, ow, rd, sa, sb, ka, kb, ra, rb, s2a, s2b, fa, fb, r2a, r2b,
                ds, dr, as_, ar, bs, br, a2s, a2r, b2s, b2r):
    n = pl.program_id(0)
    r, c, y, x, k = coords()
    near = neighbours()
    rows = t_ref.shape[0]

    @pl.when(n == 0)
    def _():
        enter({key: near[key] for key in ("k", "x", "y")})

    def d2d(m):
        return rcopy(sd.at[m], rd.at[m], ds.at[m], dr.at[m], near["k"])

    def a1(m):
        return rcopy(sa.at[m], ra.at[m], as_.at[m], ar.at[m], near["x"])

    def b1(m):
        return rcopy(sb.at[m], rb.at[m], bs.at[m], br.at[m], near["y"])

    def a2(m):
        return rcopy(s2a.at[m], r2a.at[m], a2s.at[m], a2r.at[m], near["y"])

    def b2(m):
        return rcopy(s2b.at[m], r2b.at[m], b2s.at[m], b2r.at[m], near["x"])

    @pl.when((n >= lag2) & (n < lag2 + n_chunk))
    def _():
        m = n - lag2
        a1(m).wait_recv()
        s2a[m] = ka[m, 1] + ra[m, 1]
        a2(m).start()
        fa[m] = ka[m, 0] + ra[m, 0]
        b1(m).wait_recv()
        s2b[m] = kb[m, 1] + rb[m, 1]
        b2(m).start()
        fb[m] = kb[m, 0] + rb[m, 0]

    @pl.when((n >= 1) & (n < 1 + n_chunk))
    def _():
        m = n - 1
        d2d(m).wait_recv()

        def tot(dy, dx, lo):
            b = dy * 2 + dx
            return ow[m, b, :, lo:lo + HALF] + rd[m, b, :, lo:lo + HALF]

        for dy in (0, 1):
            sa[m, dy] = tot(dy, 1, 0)
        a1(m).start()
        for dx in (0, 1):
            sb[m, dx] = tot(1, dx, HALF)
        b1(m).start()
        for dy in (0, 1):
            ka[m, dy] = tot(dy, 0, 0)
        for dx in (0, 1):
            kb[m, dx] = tot(0, dx, HALF)

    @pl.when(n < n_chunk)
    def _():
        row_id = lax.broadcasted_iota(jnp.int32, (rows, CHUNK), 0)
        seg = rows // 6
        base_row = y * (rows // 2) + 3 * (r % 4)
        for dk in (1, 0):
            half = 4 * rows
            lhs = tl_ref[dk * half:(dk + 1) * half, :]
            part = jnp.dot(lhs, v_ref[...], preferred_element_type=jnp.float32)
            part += jnp.dot(wt_ref[dk * half:(dk + 1) * half, :], t_ref[...], preferred_element_type=jnp.float32)
            for b in range(4):
                acc = part[b * rows:(b + 1) * rows]
                for i in range(3):
                    for e in range(3):
                        im_row = im_ref[dk * 4 + b, 3 * i + e:3 * i + e + 1, :]
                        acc = acc + jnp.where(row_id == base_row + seg * i + e, im_row, 0.0)
                if dk:
                    sd[n, b] = acc
                else:
                    ow[n, b] = acc
            if dk:
                d2d(n).start()

    @pl.when(n >= lag3)
    def _():
        m = n - lag3
        a2(m).wait_recv()
        col = pl.multiple_of(m * CHUNK, CHUNK)
        out_ref[:, pl.ds(col, HALF)] = fa[m] + r2a[m]
        b2(m).wait_recv()
        colb = pl.multiple_of(m * CHUNK + HALF, HALF)
        out_ref[:, pl.ds(colb, HALF)] = fb[m] + r2b[m]

    @pl.when(n == lag3 + n_chunk - 1)
    def _():
        def drain(m, carry):
            for one in (d2d, a1, b1, a2, b2):
                one(m).wait_send()
            return carry

        lax.fori_loop(0, n_chunk, drain, 0)


def ladder(tl, wt, im, v, t):
    rows, n_col = t.shape
    n_chunk = -(-n_col // CHUNK)
    lag2, lag3 = 3, 5
    depth = v.shape[0]
    last = n_chunk - 1
    dma = pltpu.SemaphoreType.DMA
    f32 = jnp.float32
    vm = lambda *s: pltpu.VMEM((n_chunk,) + s, f32)
    return pl.pallas_call(
        functools.partial(ladder_body, n_chunk, lag2, lag3),
        name="ladder_rs",
        grid=(n_chunk + lag3,),
        out_shape=jax.ShapeDtypeStruct((rows, n_chunk * CHUNK), f32),
        in_specs=[
            pl.BlockSpec((8 * rows, depth), lambda n: (0, 0)),
            pl.BlockSpec((8 * rows, rows), lambda n: (0, 0)),
            pl.BlockSpec((8, 9, CHUNK), lambda n: (0, 0, jnp.minimum(n, last))),
            pl.BlockSpec((depth, CHUNK), lambda n: (0, jnp.minimum(n, last))),
            pl.BlockSpec((rows, CHUNK), lambda n: (0, jnp.minimum(n, last))),
        ],
        out_specs=pl.BlockSpec((rows, n_chunk * CHUNK), lambda n: (0, 0)),
        scratch_shapes=[
            vm(4, rows, CHUNK), vm(4, rows, CHUNK), vm(4, rows, CHUNK),
            vm(2, rows, HALF), vm(2, rows, HALF), vm(2, rows, HALF), vm(2, rows, HALF),
            vm(2, rows, HALF), vm(2, rows, HALF),
            vm(rows, HALF), vm(rows, HALF), vm(rows, HALF), vm(rows, HALF), vm(rows, HALF), vm(rows, HALF),
        ] + [dma((n_chunk,))] * 10,
        compiler_params=pltpu.CompilerParams(
            collective_id=1, has_side_effects=True, vmem_limit_bytes=60 * 1024 * 1024,
            dimension_semantics=("arbitrary",),
        ),
        cost_estimate=pl.CostEstimate(flops=60_000_000_000, bytes_accessed=30_000_000, transcendentals=0),
    )(tl, wt, im, v, t)


def relative(a, r, axis):
    shape = a.shape
    a = a.reshape(shape[:axis] + (2, 2, 2) + shape[axis + 1:])
    for bit, ax in ((r // 4, axis), ((r // 2) % 2, axis + 1), (r % 2, axis + 2)):
        a = jnp.where(bit == 1, jnp.flip(a, ax), a)
    perm = list(range(a.ndim))
    perm[axis:axis + 3] = [axis + 2, axis, axis + 1]
    return a.transpose(perm).reshape(shape)


def solution(mesh):
    row_n = mesh.shape["row"]
    col_n = mesh.shape["col"]
    swap_z = [(0, 1), (1, 0)]

    def local_sweep(t_blk, d_blk, voovv_blk, vvvvv_blk, oooo_blk, wr_blk):
        n_occ = math.isqrt(oooo_blk.shape[1])
        n_vir = wr_blk.shape[0] // n_occ
        o_r = n_occ // row_n
        o_c = n_occ // col_n
        v_c = n_vir // col_n
        rows = o_r * n_occ
        n_col = v_c * n_vir
        piece = n_col // 4
        r, c, y, x, k = coords()
        f32 = jnp.float32

        d_rows = d_blk.reshape(o_r, 2, o_c, n_col)
        d_send = lax.dynamic_index_in_dim(d_rows, 1 - c, 1, keepdims=False)
        d_keep = lax.dynamic_index_in_dim(d_rows, c, 1, keepdims=False)
        d_recv = lax.ppermute(d_send, "col", swap_z)

        t_bf = t_blk.astype(jnp.bfloat16)
        p = t_bf.reshape(o_r, 2, o_c, 4, piece).transpose(3, 1, 0, 2, 4).reshape(4, rows, piece)
        g, zp, tl_recv = gather(p)

        tm_own = t_bf.reshape(o_r, n_occ, v_c, n_vir).transpose(0, 2, 1, 3).reshape(o_r * v_c, n_occ * n_vir)
        tm_oth = zp.reshape(4, 2, o_r, o_c, v_c // 4, n_vir).transpose(2, 0, 4, 1, 3, 5)
        tm_oth = tm_oth.reshape(o_r * v_c, n_occ * n_vir)
        r3_own = jnp.dot(tm_own, wr_blk, preferred_element_type=f32)
        r3_oth = jnp.dot(tm_oth, wr_blk, preferred_element_type=f32)

        def order(own, oth, axis):
            lo = jnp.where(c == 0, own, oth)
            hi = jnp.where(c == 0, oth, own)
            return jnp.concatenate([lo, hi], axis=axis)

        r3 = order(r3_own.reshape(o_r, v_c, o_c * n_vir), r3_oth.reshape(o_r, v_c, o_c * n_vir), 1)
        r3_t = r3.reshape(o_r, n_vir, o_c, 2, v_c).transpose(3, 2, 0, 4, 1)
        im_send = lax.dynamic_index_in_dim(r3_t, 1 - c, 0, keepdims=False).reshape(o_c, o_r, n_col)
        im_keep = lax.dynamic_index_in_dim(r3_t, c, 0, keepdims=False).reshape(o_c, o_r, n_col)
        im_recv = lax.ppermute(im_send, "col", swap_z)
        im = order(im_keep, im_recv, 0).reshape(row_n, o_r * o_r, n_col)
        im = relative(im, r, 0)

        x_part = sum(
            lax.dot_general(voovv_blk[:, q * piece:(q + 1) * piece], g[:, q].reshape(row_n * rows, piece),
                            (((1,), (1,)), ((), ())), preferred_element_type=f32)
            for q in range(4)
        )
        x_full = x_part + lax.ppermute(x_part, "col", swap_z)
        oooo = oooo_blk.reshape(rows, row_n, o_r, 2, o_c).transpose(0, 1, 3, 2, 4).reshape(rows, row_n, rows)
        oooo = relative(oooo, r, 1).reshape(rows, row_n * rows)
        w_hole = (oooo.astype(f32) + 0.5 * x_full).astype(jnp.bfloat16)

        q_own = 2 * x + k
        tl = jnp.where(y == c, lax.dynamic_index_in_dim(g, q_own, 1, keepdims=False), tl_recv)
        base = ladder(tl.reshape(row_n * rows, piece), w_hole.T, im, vvvvv_blk, t_bf)
        base = base[:, :n_col].reshape(2, o_r, o_c, n_col)
        vo_rows = voovv_blk.reshape(o_r, 2, o_c, n_col).transpose(1, 0, 2, 3)
        base = base + vo_rows.astype(f32)
        b_recv = lax.ppermute(lax.dynamic_index_in_dim(base, 1 - c, 0, keepdims=False), "col", swap_z)
        b_keep = lax.dynamic_index_in_dim(base, c, 0, keepdims=False)

        def mixed(own, oth):
            both = order(own.reshape(o_r, o_c, v_c, n_vir), oth.reshape(o_r, o_c, v_c, n_vir), 2)
            return both.transpose(0, 2, 1, 3).reshape(o_r * n_vir, o_c * n_vir)

        return (mixed(b_keep, b_recv) + r3.reshape(o_r * n_vir, o_c * n_vir)) / mixed(d_keep, d_recv)

    return jax.shard_map(
        local_sweep,
        mesh=mesh,
        in_specs=(P("row", "col"), P("row", "col"), P("row", "col"), P("row", "col"), P("row", None), P(None, "col")),
        out_specs=P("row", "col"),
        check_vma=False,
    )
```

time: 333 us -> 257 us (0.77)
  Pallas kernels: 0 us -> 121 us
  blocking collectives: 119 us -> 0 us
  waiting for transfers between devices: 73.2 us -> 23.6 us
  matrix products: 33.1 us -> 12.3 us
  between operations: 13.9 us -> 1.02 us
  other arithmetic: 15.3 us -> 19 us
    pallas_call x0 -> x2, Pallas kernels: none -> 121 us  [the longest x1 63 us: ladder(): pl.pallas_call(functools.partial(ladder_body, n_chunk, lag2, lag3), name=...]
    all_to_all x4 -> x0, blocking collectives: 119 us -> none  [the longest x1 34.7 us: local_sweep(): swap_rows = lax.all_to_all(mixed_entry, 'row', 2, 0, tiled=True)]
    all_gather x2 -> x0, waiting for transfers between devices: 73.1 us -> none  [the longest x1 46 us: local_sweep(): t_cols = lax.all_gather(t_bf, 'row', axis=0, tiled=True)]
    all_to_all x12 -> x0, local copies, waits for them, and re-layouts: 26.1 us -> none  [the longest x3 12.5 us: local_sweep(): swap_full = lax.all_to_all(swap_rows, 'col', 3, 1, tiled=True)]
    ppermute x0 -> x4, waiting for transfers between devices: none -> 23.6 us  [the longest x1 13.4 us: local_sweep(): im_recv = lax.ppermute(im_send, 'col', swap_z)]
    dot_general x4 -> x6, matrix products: 33.1 us -> 12.3 us  [the longest x4 6.47 us: local_sweep(): lax.dot_general(voovv_blk[:, q * piece:(q + 1) * piece], g[:, q].reshape(...]
    reshape x4 -> x17, local copies, waits for them, and re-layouts: 12.3 us -> 32.6 us  [the longest x2 6.48 us: mixed(): return both.transpose(0, 2, 1, 3).reshape(o_r * n_vir, o_c * n_vir)]
    unnamed x11 -> x28, local copies, waits for them, and re-layouts: 16.7 us -> 0.06 us
  transfers between devices with their start and end apart: 6 -> 4, of which waited for: 2 -> 2; matrix products, arithmetic and copies ran while one was open for 28% -> 34% of each run, Pallas kernels for 0% -> 47%
where the time goes in v1:
time: 257 us; the launch traced here: 256 us
  Pallas kernels  121 us (47%)
  local copies, waits for them, and re-layouts  71.5 us (28%)
  waiting for transfers between devices  23.6 us (9%)
  other arithmetic  19 us (7%)
  matrix products  12.3 us (5%)
  starting transfers between devices  7.43 us (3%)
    pallas_call x1, Pallas kernels, ladder(): pl.pallas_call(functools.partial(ladder_body, n_chunk, lag2, lag3), name=...  63 us
    pallas_call x1, Pallas kernels, gather(): pl.pallas_call(gather_body, name='amp_gather', out_shape=(jax.ShapeDtypeS...  58.5 us
    ppermute x1, waiting for transfers between devices, local_sweep(): im_recv = lax.ppermute(im_send, 'col', swap_z)  13.4 us
    ppermute x1, waiting for transfers between devices, local_sweep(): lax.ppermute(lax.dynamic_index_in_dim(base, 1 - c, 0, keepdims=False), 'c...  10.2 us
    reshape x2, local copies, waits for them, and re-layouts, mixed(): return both.transpose(0, 2, 1, 3).reshape(o_r * n_vir, o_c * n_vir)  6.48 us
    dot_general x4, matrix products, local_sweep(): lax.dot_general(voovv_blk[:, q * piece:(q + 1) * piece], g[:, q].reshape(...  6.47 us
    reshape x2, local copies, waits for them, and re-layouts, mixed(): oth.reshape(o_r, o_c, v_c, n_vir)  5.65 us
  transfers between devices with their start and end apart: 4, of which 2 were waited for; matrix products, arithmetic and copies ran while one was open for 34% of the time, Pallas kernels for 47%

profile of v1, /device:TPU:0, one launch (start us, length us, event | category | flops | bytes accessed | tf_op | source)
XLA Modules:
  0.0 256.3 jit_solution(9521162750557253666)
XLA Ops:
  0.0 1.5 reshape.91
  1.5 1.5 constant_dynamic-slice_fusion
  3.0 3.3 %collective-permute-start.3 = (f32[3,12,5408]{2,1,0:T(8,128)}, f32[3,12,5408]{2,1,0:T(8,128)}, u32[]{:S(2)}, u32[]{:S(2)}) collective-permute-start(f32[3,12,5408]{2,1,0:T(8,128)} %get-tuple-element.20), channel_id=1, source_target_pairs={{0,8},{8,0},{1,9},{9,1},{2,10},{10,2},{3,11},{11,3},{4,12},{12,4},... | collective-permute-start | bytes 2336264 | tf_op jit(solution)/shard_map/ppermute | solution.py:343
  6.4 0.9 reshape.76
  7.3 0.3 copy.48
  7.6 1.0 copy.49.p_ref
  8.5 58.5 %amp_gather.1 = (bf16[8,4,72,1352]{3,2,1,0:T(8,128)(2,1)}, bf16[4,72,1352]{2,1,0:T(8,128)(2,1)}, bf16[8,72,1352]{2,1,0:T(8,128)(2,1)}) custom-call(bf16[4,72,1352]{2,1,0:T(8,128)(2,1)} %copy.49.p_ref), custom_call_target="tpu_custom_call" | custom-call | flops 30000001024 | bytes 10000000 | tf_op jit(solution)/shard_map/amp_gather/pallas_call | solution.py:157
  67.0 4.6 %fusion.12 = (bf16[8,1,72,1352]{3,2,1,0:T(8,128)(2,1)S(1)}, bf16[8,1,72,1352]{3,2,1,0:T(8,128)(2,1)}, bf16[8,1,72,1352]{3,2,1,0:T(8,128)(2,1)S(1)}, bf16[8,1,72,1352]{3,2,1,0:T(8,128)(2,1)S(1)}) fusion(bf16[8,4,72,1352]{3,2,1,0:T(8,128)(2,1)} %get-tuple-element.8), kind=kLoop, calls=%fused_computation.45 | loop fusion | bytes 12460032 | tf_op jit(solution)/shard_map/slice | solution.py:369
  71.6 0.6 fusion.10
  72.3 1.3 convolution_add_fusion.2
  73.6 1.1 copy.53
  74.7 2.2 convolution_add_fusion.1
  76.9 2.3 convolution_add_fusion
  79.2 2.5 collective-permute-start
  81.7 2.2 reshape.80
  83.9 3.1 %reshape.81 = bf16[4,2,3,12,13,104]{5,4,3,2,1,0:T(8,128)(2,1)S(1)} reshape(bf16[4,72,1352]{2,1,0:T(8,128)(2,1)} %get-tuple-element.10) | data formatting | bytes 1557504 | tf_op jit(solution)/shard_map/reshape | solution.py:350
  87.1 0.3 copy.57
  87.4 2.9 %dot_general.28 = bf16[3,52,2496]{2,1,0:T(8,128)(2,1)} reshape(bf16[3,4,13,2,12,104]{5,4,3,2,1,0:T(8,128)(2,1)S(1)} %copy.57) | data formatting | bytes 1557504 | tf_op jit(solution)/shard_map/dot_general | solution.py:353
  90.2 1.1 copy.56
  91.3 2.9 %dot_general.26 = bf16[3,52,2496]{2,1,0:T(8,128)(2,1)} reshape(bf16[3,52,24,104]{3,2,1,0:T(8,128)(2,1)} %copy.56) | data formatting | bytes 1557504 | tf_op jit(solution)/shard_map/dot_general | solution.py:352
  94.2 4.5 %fusion = f32[3,52,1248]{2,1,0:T(8,128)S(1)} fusion(bf16[3,52,2496]{2,1,0:T(8,128)(2,1)} %dot_general.28, bf16[2496,1248]{1,0:T(8,128)(2,1)} %param.11), kind=kOutput, calls=%fused_computation | convolution fusion | flops 971882496 | bytes 7787520 | tf_op jit(solution)/shard_map/dot_general | solution.py:353
  98.8 1.3 broadcast_select_fusion.7
  100.3 1.8 copy.58
  102.0 2.6 %reshape.82 = f32[3,104,12,2,52]{1,4,3,2,0:T(8,128)} reshape(f32[3,104,1248]{1,2,0:T(8,128)} %copy.58) | data formatting | bytes 3115008 | tf_op jit(solution)/shard_map/reshape | solution.py:361
  104.7 2.7 %dynamic-slice_bitcast_fusion.3 = (f32[1,12,3,52,104]{4,3,0,1,2:T(8,128)}, f32[1,12,3,52,104]{4,3,0,1,2:T(8,128)S(1)}) fusion(f32[3,104,12,2,52]{1,4,3,2,0:T(8,128)} %reshape.82, s32[]{:T(128)S(6)} %select_n.160, s32[]{:T(128)S(6)} %select_n.161), kind=kLoop, calls=%fused_computation.22 | loop fusion | bytes 3115016 | tf_op jit(solution)/shard_map/jit(dynamic_index_in_dim)/dynamic_slice | solution.py:363
  107.4 1.4 reshape.84
  108.7 2.6 %reshape.102 = f32[3,2,12,5408]{3,2,1,0:T(8,128)} reshape(bf16[72,5408]{1,0:T(8,128)(2,1)} %param.8) | data formatting | bytes 2336256 | tf_op jit(solution)/shard_map/convert_element_type | solution.py:383
  111.3 0.6 dynamic-slice.6
  113.0 0.2 broadcast_select_fusion.8
  113.1 0.2 broadcast_select_fusion.9
  113.3 0.8 rev.26
  114.1 2.8 %bitcast_select_fusion = bf16[8,72,1352]{2,1,0:T(8,128)(2,1)} fusion(bf16[8,72,1352]{2,1,0:T(8,128)(2,1)} %get-tuple-element.9, bf16[8,4,72,1352]{3,2,1,0:T(8,128)(2,1)} %get-tuple-element.8, s32[]{:T(128)S(6)} %select_n.145, pred[]{:T(512)S(6)} %eq.33), kind=kLoop, calls=%fused_computation.11 | loop fusion | flops 778752 | bytes 4672517 | tf_op jit(solution)/shard_map/jit(_where)/select_n | solution.py:379
  116.9 0.2 convert_bitcast_fusion
  117.2 1.6 reshape.83
  118.8 1.8 fusion.6
  120.6 13.4 %collective-permute-done.1 = f32[12,3,5408]{2,0,1:T(8,128)} collective-permute-done((f32[12,3,5408]{2,0,1:T(8,128)}, f32[12,3,5408]{2,0,1:T(8,128)}, u32[]{:S(2)}, u32[]{:S(2)}) %collective-permute-start.1) | collective-permute-done | bytes 778784 | tf_op jit(solution)/shard_map/ppermute | solution.py:364
  134.0 1.4 broadcast_select_fusion.1
  135.3 0.2 pad_maximum_fusion.1
  135.5 1.9 copy.59
  137.4 4.0 %reshape_reshape.8 = f32[2,2,2,9,5408]{4,3,2,1,0:T(8,128)} reshape(f32[24,3,5408]{2,1,0:T(4,128)} %copy.59) | data formatting | bytes 3115008 | tf_op jit(solution)/shard_map/reshape;reshape | solution.py:315
  141.4 2.9 %reverse_select_fusion.2 = f32[2,2,2,9,5408]{4,3,2,1,0:T(8,128)S(1)} fusion(f32[2,2,2,9,5408]{4,3,2,1,0:T(8,128)} %reshape_reshape.8, pred[]{:T(512)S(6)} %eq.36), kind=kLoop, calls=%fused_computation.6 | loop fusion | flops 389376 | bytes 3115009 | tf_op jit(solution)/shard_map/jit(_where)/select_n | solution.py:317
  144.3 0.2 reverse_select_fusion.1
  144.5 0.2 fusion.4
  144.7 1.8 copy.60
  146.5 63.0 %ladder_rs.1 = f32[72,5632]{1,0:T(8,128)} custom-call(bf16[576,1352]{1,0:T(8,128)(2,1)} %bitcast.76, bf16[576,72]{1,0:T(8,128)(2,1)} %bitcast.79, f32[8,9,5408]{2,1,0:T(8,128)} %bitcast.75, bf16[1352,5408]{1,0:T(8,128)(2,1)} %v_ref.1, bf16[72,5408]{1,0:T(8,128)(2,1)} %copy-done.2), custom_call_target="tpu_custom_call" | custom-call | flops 60000002048 | bytes 30000000 | tf_op jit(solution)/shard_map/ladder_rs/pallas_call | solution.py:286
  209.5 2.7 %slice.35 = f32[72,5408]{1,0:T(8,128)} slice(f32[72,5632]{1,0:T(8,128)} %ladder_rs.1), slice={[0:72], [0:5408]} | slice | bytes 3115008 | tf_op jit(solution)/shard_map/slice | solution.py:381
  212.2 2.7 %reshape.86 = f32[2,3,12,5408]{3,2,1,0:T(8,128)} reshape(f32[72,5408]{1,0:T(8,128)} %slice.35) | data formatting | bytes 3115008 | tf_op jit(solution)/shard_map/reshape | solution.py:381
  214.9 2.4 bitcast_add_fusion
  217.4 1.6 constant_dynamic-slice_fusion.1
  219.0 1.6 collective-permute-start.2
  220.6 1.6 reshape.92
  222.1 2.9 %reshape.93 = f32[3,12,52,104]{3,2,1,0:T(8,128)} reshape(f32[3,12,5408]{2,1,0:T(8,128)} %collective-permute-done.3) | data formatting | bytes 1557504 | tf_op jit(solution)/shard_map/reshape | solution.py:388
  225.0 1.4 broadcast_select_fusion.3
  226.4 0.2 maximum_bitcast_fusion.1
  226.6 1.9 copy.63
  228.5 3.3 %reshape.94 = f32[312,1248]{1,0:T(8,128)} reshape(f32[3,104,12,104]{3,2,1,0:T(8,128)} %copy.63) | data formatting | bytes 3115008 | tf_op jit(solution)/shard_map/reshape | solution.py:389
  231.7 1.6 reshape.87
  233.3 10.2 %collective-permute-done.2 = f32[3,12,5408]{2,1,0:T(8,128)} collective-permute-done((f32[3,12,5408]{2,1,0:T(8,128)}, f32[3,12,5408]{2,1,0:T(8,128)}, u32[]{:S(2)}, u32[]{:S(2)}) %collective-permute-start.2) | collective-permute-done | bytes 778784 | tf_op jit(solution)/shard_map/ppermute | solution.py:384
  243.6 2.8 %reshape.88 = f32[3,12,52,104]{3,2,1,0:T(8,128)} reshape(f32[3,12,5408]{2,1,0:T(8,128)} %collective-permute-done.2) | data formatting | bytes 1557504 | tf_op jit(solution)/shard_map/reshape | solution.py:388
  246.3 1.4 broadcast_select_fusion.5
  247.7 0.2 maximum_bitcast_fusion
  247.9 1.9 copy.62
  249.8 3.2 %reshape.89 = f32[312,1248]{1,0:T(8,128)} reshape(f32[3,104,12,104]{3,2,1,0:T(8,128)} %copy.62) | data formatting | bytes 3115008 | tf_op jit(solution)/shard_map/reshape | solution.py:389
  253.0 3.3 %fusion.5 = f32[312,1248]{1,0:T(8,128)} fusion(f32[312,1248]{1,0:T(8,128)} %reshape.94, f32[312,1248]{1,0:T(8,128)} %reshape.89, f32[3,104,1248]{2,1,0:T(8,128)S(1)} %pad_maximum_fusion), kind=kLoop, calls=%fused_computation.14 | loop fusion | flops 778752 | bytes 6230016 | tf_op jit(solution)/shard_map/div | solution.py:391
  (39 shorter events, 0.6 us)
Async XLA Ops:
  0.0 112.6 %copy-start = (bf16[576,576]{1,0:T(8,128)(2,1)S(1)}, bf16[576,576]{1,0:T(8,128)(2,1)}, u32[]{:S(2)}) copy-start(bf16[576,576]{1,0:T(8,128)(2,1)} %param.10) | copy-start | bytes 1990660
  1.5 4.8 %copy-start.10 = (f32[72,5408]{1,0:T(8,128)S(1)}, f32[72,5408]{1,0:T(8,128)}, u32[]{:S(2)}) copy-start(f32[72,5408]{1,0:T(8,128)} %param.6) | copy-start | bytes 4672516
  3.0 219.1 %collective-permute-start.3 = (f32[3,12,5408]{2,1,0:T(8,128)}, f32[3,12,5408]{2,1,0:T(8,128)}, u32[]{:S(2)}, u32[]{:S(2)}) collective-permute-start(f32[3,12,5408]{2,1,0:T(8,128)} %get-tuple-element.20), channel_id=1, source_target_pairs={{0,8},{8,0},{1,9},{9,1},{2,10},{10,2},{3,11},{11,3},{4,12},{12,4},... | collective-permute-start | bytes 2336264 | tf_op jit(solution)/shard_map/ppermute | solution.py:343
  6.4 75.3 %copy-start.2 = (bf16[72,5408]{1,0:T(8,128)(2,1)}, bf16[72,5408]{1,0:T(8,128)(2,1)S(1)}, u32[]{:S(2)}) copy-start(bf16[72,5408]{1,0:T(8,128)(2,1)S(1)} %convert_element_type.24.t_ref) | copy-start | bytes 2336260
  67.0 4.6 %copy-start.9 = (bf16[72,5408]{1,0:T(8,128)(2,1)S(1)}, bf16[72,5408]{1,0:T(8,128)(2,1)}, u32[]{:S(2)}) copy-start(bf16[72,5408]{1,0:T(8,128)(2,1)} %param.8) | copy-start | bytes 2336260
  79.2 39.6 %collective-permute-start = (f32[72,576]{0,1:T(8,128)}, f32[72,576]{0,1:T(8,128)}, u32[]{:S(2)}, u32[]{:S(2)}) collective-permute-start(f32[72,576]{0,1:T(8,128)} %convolution_add_fusion), channel_id=1, source_target_pairs={{0,8},{8,0},{1,9},{9,1},{2,10},{10,2},{3,11},{11,3},{4,12},{12,4},... | collective-permute-start | bytes 497672 | tf_op jit(solution)/shard_map/ppermute | solution.py:373
  87.4 2.9 %copy-start.8 = (bf16[3,24,52,104]{3,2,1,0:T(8,128)(2,1)S(1)}, bf16[3,24,52,104]{3,2,1,0:T(8,128)(2,1)}, u32[]{:S(2)}) copy-start(bf16[3,24,52,104]{3,2,1,0:T(8,128)(2,1)} %reshape.80) | copy-start | bytes 2336260
  91.3 7.4 %slice-start = ((s8[6389760]{0:T(1024)(128)(4,1)}), s8[2195456]{0:T(1024)(128)(4,1)S(1)}, s32[]{:S(2)}) async-start(s8[6389760]{0:T(1024)(128)(4,1)} %bitcast.66), calls=%async_computation | async-start | bytes 4390912
  94.2 4.6 %slice-start.1 = ((s8[6389760]{0:T(1024)(128)(4,1)}), s8[4194304]{0:T(1024)(128)(4,1)S(1)}, s32[]{:S(2)}) async-start(s8[6389760]{0:T(1024)(128)(4,1)} %bitcast.66), calls=%async_computation.1 | async-start | bytes 8388608
  94.2 4.6 %copy-start.3 = (bf16[3,52,2496]{2,1,0:T(8,128)(2,1)S(1)}, bf16[3,52,2496]{2,1,0:T(8,128)(2,1)}, u32[]{:S(2)}) copy-start(bf16[3,52,2496]{2,1,0:T(8,128)(2,1)} %dot_general.26) | copy-start | bytes 2336260
  108.7 2.6 %copy-start.11 = (u32[16]{0:T(128)S(1)}, u32[16]{0:T(128)}, u32[]{:S(2)}) copy-start(u32[16]{0:T(128)} %constant.91) | copy-start | bytes 196
  108.7 25.2 %collective-permute-start.1 = (f32[12,3,5408]{2,0,1:T(8,128)}, f32[12,3,5408]{2,0,1:T(8,128)}, u32[]{:S(2)}, u32[]{:S(2)}) collective-permute-start(f32[12,3,5408]{2,0,1:T(8,128)} %reshape.84), channel_id=1, source_target_pairs={{0,8},{8,0},{1,9},{9,1},{2,10},{10,2},{3,11},{11,3},{4,12},{12,4},... | collective-permute-start | bytes 2336264 | tf_op jit(solution)/shard_map/ppermute | solution.py:364
  217.3 3.2 %copy-start.4 = (f32[3,1,12,5408]{3,2,1,0:T(8,128)S(1)}, f32[3,1,12,5408]{3,2,1,0:T(8,128)}, u32[]{:S(2)}) copy-start(f32[3,1,12,5408]{3,2,1,0:T(8,128)} %get-tuple-element.19) | copy-start | bytes 2336260
  219.0 24.6 %collective-permute-start.2 = (f32[3,12,5408]{2,1,0:T(8,128)}, f32[3,12,5408]{2,1,0:T(8,128)}, u32[]{:S(2)}, u32[]{:S(2)}) collective-permute-start(f32[3,12,5408]{2,1,0:T(8,128)} %get-tuple-element.16), channel_id=1, source_target_pairs={{0,8},{8,0},{1,9},{9,1},{2,10},{10,2},{3,11},{11,3},{4,12},{12,4},... | collective-permute-start | bytes 2336264 | tf_op jit(solution)/shard_map/ppermute | solution.py:384
  222.1 2.9 %copy-start.7 = (f32[3,12,52,104]{3,2,1,0:T(8,128)S(1)}, f32[3,12,52,104]{3,2,1,0:T(8,128)}, u32[]{:S(2)}) copy-start(f32[3,12,52,104]{3,2,1,0:T(8,128)} %reshape.92) | copy-start | bytes 2336260
  228.4 3.3 %copy-start.5 = (f32[1,3,12,5408]{3,2,1,0:T(8,128)S(1)}, f32[1,3,12,5408]{3,2,1,0:T(8,128)}, u32[]{:S(2)}) copy-start(f32[1,3,12,5408]{3,2,1,0:T(8,128)} %get-tuple-element.15) | copy-start | bytes 2336260
  233.3 13.0 %copy-start.6 = (f32[3,12,52,104]{3,2,1,0:T(8,128)S(1)}, f32[3,12,52,104]{3,2,1,0:T(8,128)}, u32[]{:S(2)}) copy-start(f32[3,12,52,104]{3,2,1,0:T(8,128)} %reshape.87) | copy-start | bytes 2336260
  249.8 6.5 %copy-start.1 = (bf16[576,576]{1,0:T(8,128)(2,1)S(1)}, bf16[576,576]{1,0:T(8,128)(2,1)}, u32[]{:S(2)}) copy-start(bf16[576,576]{1,0:T(8,128)(2,1)} %param.10) | copy-start | bytes 1990660

commit v2 on v1

--- a/solution.py
+++ b/solution.py
@@ -172,17 +172,15 @@
     )(p)
 
 
-def ladder_body(n_chunk, lag2, lag3, tl_ref, wt_ref, im_ref, v_ref, t_ref, out_ref,
-                sd, ow, rd, sa, sb, ka, kb, ra, rb, s2a, s2b, fa, fb, r2a, r2b,
-                ds, dr, as_, ar, bs, br, a2s, a2r, b2s, b2r):
+def ladder_body(n_chunk, lag2, lag3, tl_ref, wt_ref, v_ref, t_ref, vo_ref, im_ref, d_ref, base_ref, brecv_ref, drecv_ref,
+                sd, ow, rd, sa, sb, ka, kb, ra, rb, s2a, s2b, fa, fb, r2a, r2b, fin, imv,
+                ds, dr, as_, ar, bs, br, a2s, a2r, b2s, b2r, zs, zr, ims, imr, dds, ddr, iml):
     n = pl.program_id(0)
     r, c, y, x, k = coords()
     near = neighbours()
     rows = t_ref.shape[0]
-
-    @pl.when(n == 0)
-    def _():
-        enter({key: near[key] for key in ("k", "x", "y")})
+    win = brecv_ref.shape[0]
+    dwin = drecv_ref.shape[0] // 3
 
     def d2d(m):
         return rcopy(sd.at[m], rd.at[m], ds.at[m], dr.at[m], near["k"])
@@ -198,6 +196,33 @@
 
     def b2(m):
         return rcopy(s2b.at[m], r2b.at[m], b2s.at[m], b2r.at[m], near["x"])
+
+    def zb(m):
+        off = pl.multiple_of((rows - win) * (1 - c), 8)
+        col = pl.multiple_of(m * CHUNK, CHUNK)
+        return rcopy(fin.at[m, pl.ds(off, win)], brecv_ref.at[:, pl.ds(col, CHUNK)], zs.at[m], zr.at[m], near["z"])
+
+    def zim(m):
+        return rcopy(im_ref.at[1 - c, m], imv.at[c, m], ims.at[m], imr.at[m], near["z"])
+
+    def zim_in(m):
+        return rcopy(im_ref.at[1 - c, m], imv.at[1 - c, m], ims.at[m], imr.at[m], near["z"])
+
+    def im_own():
+        return pltpu.make_async_copy(im_ref.at[c], imv.at[c], iml.at[0])
+
+    def zd(i):
+        off = pl.multiple_of(i * (rows // 3) + 8 * (1 - c), 8)
+        return rcopy(d_ref.at[pl.ds(off, dwin)], drecv_ref.at[pl.ds(i * dwin, dwin)], dds.at[i], ddr.at[i], near["z"])
+
+    @pl.when(n == 0)
+    def _():
+        enter(near)
+        im_own().start()
+        for m in range(n_chunk):
+            zim(m).start()
+        for i in range(3):
+            zd(i).start()
 
     @pl.when((n >= lag2) & (n < lag2 + n_chunk))
     def _():
@@ -231,8 +256,13 @@
         for dx in (0, 1):
             kb[m, dx] = tot(0, dx, HALF)
 
+    @pl.when(n == 0)
+    def _():
+        im_own().wait()
+
     @pl.when(n < n_chunk)
     def _():
+        zim_in(n).wait_recv()
         row_id = lax.broadcasted_iota(jnp.int32, (rows, CHUNK), 0)
         seg = rows // 6
         base_row = y * (rows // 2) + 3 * (r % 4)
@@ -241,16 +271,20 @@
             lhs = tl_ref[dk * half:(dk + 1) * half, :]
             part = jnp.dot(lhs, v_ref[...], preferred_element_type=jnp.float32)
             part += jnp.dot(wt_ref[dk * half:(dk + 1) * half, :], t_ref[...], preferred_element_type=jnp.float32)
-            for b in range(4):
-                acc = part[b * rows:(b + 1) * rows]
-                for i in range(3):
-                    for e in range(3):
-                        im_row = im_ref[dk * 4 + b, 3 * i + e:3 * i + e + 1, :]
-                        acc = acc + jnp.where(row_id == base_row + seg * i + e, im_row, 0.0)
-                if dk:
-                    sd[n, b] = acc
-                else:
-                    ow[n, b] = acc
+            for dy in (0, 1):
+                y_b = y + dy * (1 - 2 * y)
+                for dx in (0, 1):
+                    b = dy * 2 + dx
+                    bl = 2 * (x + dx * (1 - 2 * x)) + k + dk * (1 - 2 * k)
+                    acc = part[b * rows:(b + 1) * rows]
+                    for i in range(3):
+                        for e in range(3):
+                            im_row = imv[y_b, n, pl.ds(e * seg + 3 * bl + i, 1), :]
+                            acc = acc + jnp.where(row_id == base_row + seg * i + e, im_row, 0.0)
+                    if dk:
+                        sd[n, b] = acc
+                    else:
+                        ow[n, b] = acc
             if dk:
                 d2d(n).start()
 
@@ -258,56 +292,114 @@
     def _():
         m = n - lag3
         a2(m).wait_recv()
-        col = pl.multiple_of(m * CHUNK, CHUNK)
-        out_ref[:, pl.ds(col, HALF)] = fa[m] + r2a[m]
+        fin[m, :, 0:HALF] = fa[m] + r2a[m] + vo_ref[:, 0:HALF].astype(jnp.float32)
         b2(m).wait_recv()
-        colb = pl.multiple_of(m * CHUNK + HALF, HALF)
-        out_ref[:, pl.ds(colb, HALF)] = fb[m] + r2b[m]
+        fin[m, :, HALF:CHUNK] = fb[m] + r2b[m] + vo_ref[:, HALF:CHUNK].astype(jnp.float32)
+        zb(m).start()
+        base_ref[:, pl.ds(pl.multiple_of(m * CHUNK, CHUNK), CHUNK)] = fin[m]
 
     @pl.when(n == lag3 + n_chunk - 1)
     def _():
         def drain(m, carry):
-            for one in (d2d, a1, b1, a2, b2):
+            for one in (d2d, a1, b1, a2, b2, zb, zim):
                 one(m).wait_send()
+            zb(m).wait_recv()
             return carry
 
         lax.fori_loop(0, n_chunk, drain, 0)
-
-
-def ladder(tl, wt, im, v, t):
+        for i in range(3):
+            zd(i).wait_send()
+            zd(i).wait_recv()
+
+
+def ladder(tl, wt, v, t, vo, im, d):
     rows, n_col = t.shape
     n_chunk = -(-n_col // CHUNK)
     lag2, lag3 = 3, 5
     depth = v.shape[0]
     last = n_chunk - 1
+    win = im.shape[2]
+    dwin = 16
+    wide = n_chunk * CHUNK
     dma = pltpu.SemaphoreType.DMA
     f32 = jnp.float32
     vm = lambda *s: pltpu.VMEM((n_chunk,) + s, f32)
+    any_spec = pl.BlockSpec(memory_space=pl.ANY)
     return pl.pallas_call(
         functools.partial(ladder_body, n_chunk, lag2, lag3),
         name="ladder_rs",
         grid=(n_chunk + lag3,),
-        out_shape=jax.ShapeDtypeStruct((rows, n_chunk * CHUNK), f32),
+        out_shape=(
+            jax.ShapeDtypeStruct((rows, wide), f32),
+            jax.ShapeDtypeStruct((win, wide), f32),
+            jax.ShapeDtypeStruct((3 * dwin, n_col), f32),
+        ),
         in_specs=[
             pl.BlockSpec((8 * rows, depth), lambda n: (0, 0)),
             pl.BlockSpec((8 * rows, rows), lambda n: (0, 0)),
-            pl.BlockSpec((8, 9, CHUNK), lambda n: (0, 0, jnp.minimum(n, last))),
             pl.BlockSpec((depth, CHUNK), lambda n: (0, jnp.minimum(n, last))),
             pl.BlockSpec((rows, CHUNK), lambda n: (0, jnp.minimum(n, last))),
+            pl.BlockSpec((rows, CHUNK), lambda n: (0, jnp.maximum(n - lag3, 0))),
+            any_spec,
+            any_spec,
         ],
-        out_specs=pl.BlockSpec((rows, n_chunk * CHUNK), lambda n: (0, 0)),
+        out_specs=(pl.BlockSpec((rows, wide), lambda n: (0, 0)), any_spec, any_spec),
         scratch_shapes=[
             vm(4, rows, CHUNK), vm(4, rows, CHUNK), vm(4, rows, CHUNK),
             vm(2, rows, HALF), vm(2, rows, HALF), vm(2, rows, HALF), vm(2, rows, HALF),
             vm(2, rows, HALF), vm(2, rows, HALF),
             vm(rows, HALF), vm(rows, HALF), vm(rows, HALF), vm(rows, HALF), vm(rows, HALF), vm(rows, HALF),
-        ] + [dma((n_chunk,))] * 10,
+            vm(rows, CHUNK), pltpu.VMEM((2, n_chunk, win, CHUNK), f32),
+        ] + [dma((n_chunk,))] * 14 + [dma((3,)), dma((3,)), dma((1,))],
         compiler_params=pltpu.CompilerParams(
             collective_id=1, has_side_effects=True, vmem_limit_bytes=60 * 1024 * 1024,
             dimension_semantics=("arbitrary",),
         ),
         cost_estimate=pl.CostEstimate(flops=60_000_000_000, bytes_accessed=30_000_000, transcendentals=0),
-    )(tl, wt, im, v, t)
+    )(tl, wt, v, t, vo, im, d)
+
+
+def finish_body(n_vir, base_ref, brecv_ref, d_ref, drecv_ref, r3_ref, out_ref, sb, sd):
+    c = lax.axis_index("col")
+    rows = base_ref.shape[0]
+    win = brecv_ref.shape[0]
+    dwin = drecv_ref.shape[0] // 3
+    o_c = rows // 6
+    v_c = n_vir // 2
+    off = pl.multiple_of((rows - win) * c, 8)
+    for a in range(v_c):
+        lanes = slice(a * n_vir, (a + 1) * n_vir)
+        sb[c, a * win:(a + 1) * win, 0:n_vir] = base_ref[pl.ds(off, win), lanes]
+        sb[1 - c, a * win:(a + 1) * win, 0:n_vir] = brecv_ref[:, lanes]
+        for i in range(3):
+            at = (a * 3 + i) * dwin
+            sd[c, at:at + dwin, 0:n_vir] = d_ref[pl.ds(pl.multiple_of(i * (rows // 3) + 8 * c, 8), dwin), lanes]
+            sd[1 - c, at:at + dwin, 0:n_vir] = drecv_ref[i * dwin:(i + 1) * dwin, lanes]
+    for h in range(2):
+        for i in range(3):
+            out_rows = slice(i * n_vir + h * v_c, i * n_vir + (h + 1) * v_c)
+            for j in range(o_c):
+                cols = slice(j * n_vir, (j + 1) * n_vir)
+                num = sb[h, pl.ds(4 * c + i * o_c + j, v_c, stride=win), :]
+                den = sd[h, pl.ds(4 * c + i * dwin + j, v_c, stride=3 * dwin), :]
+                out_ref[out_rows, cols] = (num[:, 0:n_vir] + r3_ref[out_rows, cols]) / den[:, 0:n_vir]
+
+
+def finish(base, brecv, d, drecv, r3, n_vir):
+    v_c = n_vir // 2
+    f32 = jnp.float32
+    return pl.pallas_call(
+        functools.partial(finish_body, n_vir),
+        name="finish",
+        out_shape=jax.ShapeDtypeStruct(r3.shape, f32),
+        in_specs=[pl.BlockSpec(memory_space=pltpu.VMEM)] * 5,
+        out_specs=pl.BlockSpec(memory_space=pltpu.VMEM),
+        scratch_shapes=[
+            pltpu.VMEM((2, v_c * brecv.shape[0], 128), f32),
+            pltpu.VMEM((2, v_c * drecv.shape[0], 128), f32),
+        ],
+        compiler_params=pltpu.CompilerParams(vmem_limit_bytes=60 * 1024 * 1024),
+    )(base, brecv, d, drecv, r3)
 
 
 def relative(a, r, axis):
@@ -337,13 +429,10 @@
         r, c, y, x, k = coords()
         f32 = jnp.float32
 
-        d_rows = d_blk.reshape(o_r, 2, o_c, n_col)
-        d_send = lax.dynamic_index_in_dim(d_rows, 1 - c, 1, keepdims=False)
-        d_keep = lax.dynamic_index_in_dim(d_rows, c, 1, keepdims=False)
-        d_recv = lax.ppermute(d_send, "col", swap_z)
-
         t_bf = t_blk.astype(jnp.bfloat16)
-        p = t_bf.reshape(o_r, 2, o_c, 4, piece).transpose(3, 1, 0, 2, 4).reshape(4, rows, piece)
+        t_perm = t_bf.reshape(o_r, 2, o_c, n_col).transpose(1, 0, 2, 3).reshape(rows, n_col)
+        p = t_perm.reshape(rows, 4, piece).transpose(1, 0, 2)
+        vo_perm = voovv_blk.reshape(o_r, 2, o_c, n_col).transpose(1, 0, 2, 3).reshape(rows, n_col)
         g, zp, tl_recv = gather(p)
 
         tm_own = t_bf.reshape(o_r, n_occ, v_c, n_vir).transpose(0, 2, 1, 3).reshape(o_r * v_c, n_occ * n_vir)
@@ -358,37 +447,26 @@
             return jnp.concatenate([lo, hi], axis=axis)
 
         r3 = order(r3_own.reshape(o_r, v_c, o_c * n_vir), r3_oth.reshape(o_r, v_c, o_c * n_vir), 1)
-        r3_t = r3.reshape(o_r, n_vir, o_c, 2, v_c).transpose(3, 2, 0, 4, 1)
-        im_send = lax.dynamic_index_in_dim(r3_t, 1 - c, 0, keepdims=False).reshape(o_c, o_r, n_col)
-        im_keep = lax.dynamic_index_in_dim(r3_t, c, 0, keepdims=False).reshape(o_c, o_r, n_col)
-        im_recv = lax.ppermute(im_send, "col", swap_z)
-        im = order(im_keep, im_recv, 0).reshape(row_n, o_r * o_r, n_col)
-        im = relative(im, r, 0)
+        r3_t = r3.reshape(o_r, n_vir, o_c, 2, v_c).transpose(3, 0, 2, 4, 1).reshape(2, o_r * o_c, n_col)
+        wide = -(-n_col // CHUNK) * CHUNK
+        im = jnp.pad(r3_t, ((0, 0), (0, 4), (0, wide - n_col)))
+        im = im.reshape(2, rows // 2 + 4, wide // CHUNK, CHUNK).transpose(0, 2, 1, 3)
 
         x_part = sum(
-            lax.dot_general(voovv_blk[:, q * piece:(q + 1) * piece], g[:, q].reshape(row_n * rows, piece),
+            lax.dot_general(vo_perm[:, q * piece:(q + 1) * piece], g[:, q].reshape(row_n * rows, piece),
                             (((1,), (1,)), ((), ())), preferred_element_type=f32)
             for q in range(4)
         )
         x_full = x_part + lax.ppermute(x_part, "col", swap_z)
-        oooo = oooo_blk.reshape(rows, row_n, o_r, 2, o_c).transpose(0, 1, 3, 2, 4).reshape(rows, row_n, rows)
-        oooo = relative(oooo, r, 1).reshape(rows, row_n * rows)
+        oooo = oooo_blk.reshape(o_r, 2, o_c, row_n, o_r, 2, o_c).transpose(1, 0, 2, 3, 5, 4, 6)
+        oooo = relative(oooo.reshape(rows, row_n, rows), r, 1).reshape(rows, row_n * rows)
         w_hole = (oooo.astype(f32) + 0.5 * x_full).astype(jnp.bfloat16)
 
         q_own = 2 * x + k
         tl = jnp.where(y == c, lax.dynamic_index_in_dim(g, q_own, 1, keepdims=False), tl_recv)
-        base = ladder(tl.reshape(row_n * rows, piece), w_hole.T, im, vvvvv_blk, t_bf)
-        base = base[:, :n_col].reshape(2, o_r, o_c, n_col)
-        vo_rows = voovv_blk.reshape(o_r, 2, o_c, n_col).transpose(1, 0, 2, 3)
-        base = base + vo_rows.astype(f32)
-        b_recv = lax.ppermute(lax.dynamic_index_in_dim(base, 1 - c, 0, keepdims=False), "col", swap_z)
-        b_keep = lax.dynamic_index_in_dim(base, c, 0, keepdims=False)
-
-        def mixed(own, oth):
-            both = order(own.reshape(o_r, o_c, v_c, n_vir), oth.reshape(o_r, o_c, v_c, n_vir), 2)
-            return both.transpose(0, 2, 1, 3).reshape(o_r * n_vir, o_c * n_vir)
-
-        return (mixed(b_keep, b_recv) + r3.reshape(o_r * n_vir, o_c * n_vir)) / mixed(d_keep, d_recv)
+        base, brecv, drecv = ladder(
+            tl.reshape(row_n * rows, piece), w_hole.T, vvvvv_blk, t_perm, vo_perm, im, d_blk)
+        return finish(base, brecv, d_blk, drecv, r3.reshape(o_r * n_vir, o_c * n_vir), n_vir)
 
     return jax.shard_map(
         local_sweep,

time: 257 us -> 208 us (0.81)
  waiting for transfers between devices: 23.6 us -> 0.01 us
  local copies, waits for them, and re-layouts: 71.5 us -> 50.1 us
  Pallas kernels: 121 us -> 134 us
  other arithmetic: 19 us -> 6.4 us
  starting transfers between devices: 7.43 us -> 2.5 us
    ppermute x3 -> x0, waiting for transfers between devices: 23.6 us -> none  [the longest x1 13.4 us: local_sweep(): im_recv = lax.ppermute(im_send, 'col', swap_z)]
    pallas_call x0 -> x1, Pallas kernels: none -> 11.7 us  [finish(): pl.pallas_call(functools.partial(finish_body, n_vir), name='finish', out_...]
    reshape x15 -> x9, local copies, waits for them, and re-layouts: 27.3 us -> 17.7 us  [the longest x2 6.2 us: local_sweep(): r3.reshape(o_r, n_vir, o_c, 2, v_c).transpose(3, 0, 2, 4, 1)]
    pallas_call x1, Pallas kernels: 63 us -> 71 us  [ladder(): pl.pallas_call(functools.partial(ladder_body, n_chunk, lag2, lag3), name=...]
    pallas_call x1, Pallas kernels: 58.5 us -> 51.6 us  [gather(): pl.pallas_call(gather_body, name='amp_gather', out_shape=(jax.ShapeDtypeS...]
    dynamic_slice x3 -> x0, local copies, waits for them, and re-layouts: 5.76 us -> none  [the longest x1 2.69 us: local_sweep(): lax.dynamic_index_in_dim(r3_t, c, 0, keepdims=False)]
    ppermute x3 -> x0, starting transfers between devices: 4.94 us -> none  [the longest x1 3.31 us: local_sweep(): d_recv = lax.ppermute(d_send, 'col', swap_z)]
    select_n x3 -> x0, other arithmetic: 4.1 us -> none  [order(): lo = jnp.where(c == 0, own, oth)]
  transfers between devices with their start and end apart: 4 -> 1, of which waited for: 2 -> 0; matrix products, arithmetic and copies ran while one was open for 34% -> 20% of each run, Pallas kernels for 47% -> 0%
where the time goes in v2:
time: 208 us; the launch traced here: 207 us
  Pallas kernels  134 us (64%)
  local copies, waits for them, and re-layouts  50.1 us (24%)
  matrix products  13.1 us (6%)
  other arithmetic  6.4 us (3%)
  starting transfers between devices  2.5 us (1%)
    pallas_call x1, Pallas kernels, ladder(): pl.pallas_call(functools.partial(ladder_body, n_chunk, lag2, lag3), name=...  71 us
    pallas_call x1, Pallas kernels, gather(): pl.pallas_call(gather_body, name='amp_gather', out_shape=(jax.ShapeDtypeS...  51.6 us
    pallas_call x1, Pallas kernels, finish(): pl.pallas_call(functools.partial(finish_body, n_vir), name='finish', out_...  11.7 us
    dot_general x4, matrix products, local_sweep(): lax.dot_general(vo_perm[:, q * piece:(q + 1) * piece], g[:, q].reshape(ro...  7.27 us
    reshape x2, local copies, waits for them, and re-layouts, local_sweep(): r3.reshape(o_r, n_vir, o_c, 2, v_c).transpose(3, 0, 2, 4, 1)  6.2 us
    slice x1, local copies, waits for them, and re-layouts, local_sweep(): g[:, q].reshape(row_n * rows, piece)  5.83 us
    reshape x2, local copies, waits for them, and re-layouts, local_sweep(): im.reshape(2, rows // 2 + 4, wide // CHUNK, CHUNK).transpose(0, 2, 1, 3)  5.2 us
    dot_general x1, matrix products, local_sweep(): r3_oth = jnp.dot(tm_oth, wr_blk, preferred_element_type=f32)  4.53 us
  transfers between devices with their start and end apart: 1, of which 0 were waited for; matrix products, arithmetic and copies ran while one was open for 20% of the time, Pallas kernels for 0%

profile of v2, /device:TPU:0, one launch (start us, length us, event | category | flops | bytes accessed | tf_op | source)
XLA Modules:
  0.0 207.3 jit_solution(7361644479598124582)
XLA Ops:
  0.0 0.0 copy-start
  0.0 1.6 convert_element_type.17
  1.6 1.2 reshape.48
  2.8 1.3 copy.43
  4.1 1.1 reshape_reshape.7
  5.1 1.0 copy.64
  6.1 51.6 %amp_gather.1 = (bf16[8,4,72,1352]{3,2,1,0:T(8,128)(2,1)}, bf16[4,72,1352]{2,1,0:T(8,128)(2,1)}, bf16[8,72,1352]{2,1,0:T(8,128)(2,1)}) custom-call(bf16[4,72,1352]{2,1,0:T(8,128)(2,1)} %bitcast.66), custom_call_target="tpu_custom_call" | custom-call | flops 30000001024 | bytes 10000000 | tf_op jit(solution)/shard_map/amp_gather/pallas_call | solution.py:157
  57.7 0.0 copy-start.9
  57.7 5.8 %fusion.10 = (bf16[8,1,72,1352]{3,2,1,0:T(8,128)(2,1)}, bf16[8,1,72,1352]{3,2,1,0:T(8,128)(2,1)}, bf16[8,1,72,1352]{3,2,1,0:T(8,128)(2,1)}, bf16[8,1,72,1352]{3,2,1,0:T(8,128)(2,1)}) fusion(bf16[8,4,72,1352]{3,2,1,0:T(8,128)(2,1)} %get-tuple-element.11), kind=kLoop, calls=%fused_computation.25 | loop fusion | bytes 12460032 | tf_op jit(solution)/shard_map/slice | solution.py:456
  63.5 0.0 copy-done.9
  63.5 1.2 reshape.51
  64.7 2.3 %copy.47 = bf16[2,3,12,5408]{3,2,1,0:T(8,128)(2,1)} copy(bf16[2,3,12,5408]{3,2,0,1:T(8,128)(2,1)} %bitcast.61) | data formatting | bytes 1557504 | tf_op jit(solution)/shard_map/transpose | solution.py:435
  67.0 1.6 reshape.52.vo_ref
  68.6 0.0 copy-start.6
  68.6 0.0 copy-start.4
  68.6 2.4 %fusion.8 = f32[72,576]{1,0:T(8,128)S(1)} fusion(bf16[576,1352]{1,0:T(8,128)(2,1)} %bitcast.58, bf16[72,5408]{1,0:T(8,128)(2,1)S(1)} %reshape.52.vo_ref), kind=kOutput, calls=%fused_computation.22 | convolution fusion | flops 112140288 | bytes 1926144 | tf_op jit(solution)/shard_map/dot_general | solution.py:456
  70.9 0.0 copy-done.4
  71.0 1.3 convolution_add_fusion.2
  72.3 1.8 copy.48
  74.1 0.0 copy-start.3
  74.1 2.2 %convolution_add_fusion.1 = f32[72,576]{0,1:T(8,128)S(1)} fusion(f32[72,576]{0,1:T(8,128)} %copy.48, bf16[576,1352]{1,0:T(8,128)(2,1)} %bitcast.56, bf16[72,5408]{1,0:T(8,128)(2,1)S(1)} %reshape.52.vo_ref), kind=kOutput, calls=%fused_computation.8 | convolution fusion | flops 112181760 | bytes 2092032 | tf_op jit(solution)/shard_map/dot_general | solution.py:456
  76.3 0.0 copy-done.6
  76.3 0.0 copy-done.3
  76.3 1.4 convolution_add_fusion
  77.7 2.5 %collective-permute-start = (f32[72,576]{0,1:T(8,128)}, f32[72,576]{0,1:T(8,128)}, u32[]{:S(2)}, u32[]{:S(2)}) collective-permute-start(f32[72,576]{0,1:T(8,128)} %convolution_add_fusion), channel_id=1, source_target_pairs={{0,8},{8,0},{1,9},{9,1},{2,10},{10,2},{3,11},{11,3},{4,12},{12,4},... | collective-permute-start | bytes 497672 | tf_op jit(solution)/shard_map/ppermute | solution.py:460
  80.2 1.3 reshape.53.t_ref
  81.5 2.2 %reshape.54 = bf16[3,24,52,104]{3,2,1,0:T(8,128)(2,1)} reshape(bf16[72,5408]{1,0:T(8,128)(2,1)S(1)} %convert_element_type.17) | data formatting | bytes 1557504 | tf_op jit(solution)/shard_map/reshape | solution.py:438
  83.7 0.0 copy-done.10
  83.7 0.6 dynamic-slice
  85.0 0.0 copy-done
  85.0 1.1 reshape.50
  86.1 0.5 copy.45
  86.6 0.7 reshape_reshape.8
  87.3 0.0 copy-start.8
  87.4 0.1 copy.46
  87.6 0.9 copy-done.8
  88.4 2.0 reshape.55
  90.5 0.3 copy.53
  90.8 2.9 %dot_general.28 = bf16[3,52,2496]{2,1,0:T(8,128)(2,1)} reshape(bf16[3,4,13,2,12,104]{5,4,3,2,1,0:T(8,128)(2,1)S(1)} %copy.53) | data formatting | bytes 1557504 | tf_op jit(solution)/shard_map/dot_general | solution.py:442
  93.6 2.5 %copy.52 = bf16[3,52,24,104]{3,2,1,0:T(8,128)(2,1)} copy(bf16[3,52,24,104]{3,1,2,0:T(8,128)(2,1)} %bitcast.62) | data formatting | bytes 1557504 | tf_op jit(solution)/shard_map/transpose | solution.py:438
  96.1 2.7 %dot_general.26 = bf16[3,52,2496]{2,1,0:T(8,128)(2,1)} reshape(bf16[3,52,24,104]{3,2,1,0:T(8,128)(2,1)} %copy.52) | data formatting | bytes 1557504 | tf_op jit(solution)/shard_map/dot_general | solution.py:441
  98.9 4.5 %fusion = f32[3,52,1248]{2,1,0:T(8,128)S(1)} fusion(bf16[3,52,2496]{2,1,0:T(8,128)(2,1)} %dot_general.28, bf16[2496,1248]{1,0:T(8,128)(2,1)} %param.11), kind=kOutput, calls=%fused_computation | convolution fusion | flops 971882496 | bytes 7787520 | tf_op jit(solution)/shard_map/dot_general | solution.py:442
  103.4 0.0 copy-done.7
  103.4 0.0 copy-start.5
  103.4 2.8 %bitcast_select_fusion = bf16[8,72,1352]{2,1,0:T(8,128)(2,1)} fusion(bf16[8,72,1352]{2,1,0:T(8,128)(2,1)S(1)} %copy-done.7, bf16[8,4,72,1352]{3,2,1,0:T(8,128)(2,1)} %get-tuple-element.11, s32[]{:T(128)S(6)} %select_n.73, pred[]{:T(512)S(6)} %eq.21), kind=kLoop, calls=%fused_computation.5 | loop fusion | flops 778752 | bytes 4672517 | tf_op jit(solution)/shard_map/jit(_where)/select_n | solution.py:466
  106.3 0.0 slice-done
  106.3 0.0 slice-done.1
  106.3 0.0 copy-done.5
  106.3 1.3 broadcast_select_fusion.1
  107.6 0.1 pad_maximum_fusion
  107.8 0.0 copy-start.2
  107.8 1.8 copy.54
  109.6 0.0 copy-done.2
  109.6 2.6 %reshape.56 = f32[3,104,12,2,52]{1,4,3,2,0:T(8,128)} reshape(f32[3,104,1248]{1,2,0:T(8,128)} %copy.54) | data formatting | bytes 3115008 | tf_op jit(solution)/shard_map/reshape | solution.py:450
  112.2 3.6 %reshape.57 = f32[2,36,5408]{2,0,1:T(2,128)S(1)} reshape(f32[2,3,12,52,104]{4,3,0,2,1:T(8,128)} %bitcast.54) | data formatting | bytes 3115008 | tf_op jit(solution)/shard_map/reshape | solution.py:450
  115.8 1.8 pad.4
  117.6 2.9 %reshape.70 = f32[2,40,11,512]{3,2,0,1:T(8,128)S(1)} reshape(f32[2,40,5632]{2,0,1:T(2,128)} %pad.4) | data formatting | bytes 3604480 | tf_op jit(solution)/shard_map/reshape | solution.py:453
  120.5 2.3 %copy.63 = f32[2,40,11,512]{3,1,2,0:T(8,128)} copy(f32[2,40,11,512]{3,2,0,1:T(8,128)S(1)} %reshape.70) | data formatting | bytes 3604480 | tf_op jit(solution)/shard_map/reshape | solution.py:453
  122.8 0.0 collective-permute-done
  122.8 1.8 fusion.4
  124.6 71.0 %ladder_rs.1 = (f32[72,5632]{1,0:T(8,128)}, f32[40,5632]{1,0:T(8,128)}, f32[48,5408]{1,0:T(8,128)}) custom-call(bf16[576,1352]{1,0:T(8,128)(2,1)} %bitcast.65, bf16[576,72]{1,0:T(8,128)(2,1)} %bitcast.67, bf16[1352,5408]{1,0:T(8,128)(2,1)} %v_ref.1, bf16[72,5408]{1,0:T(8,128)(2,1)} %reshape.53.t_ref, bf16[72,5408]{1,0:T(8,128)(2,1)} %copy-done.6, ...), custom_call_target="tpu_custom_call" | custom-call | flops 60000002048 | bytes 30000000 | tf_op jit(solution)/shard_map/ladder_rs/pallas_call | solution.py:328
  195.6 0.0 copy-start.1
  195.6 11.7 %finish.1 = f32[312,1248]{1,0:T(8,128)} custom-call(f32[72,5632]{1,0:T(8,128)} %get-tuple-element.14.base_ref, f32[40,5632]{1,0:T(8,128)} %get-tuple-element.15.brecv_ref, f32[72,5408]{1,0:T(8,128)} %d_ref.3, f32[48,5408]{1,0:T(8,128)} %get-tuple-element.16.drecv_ref, f32[312,1248]{1,0:T(8,128)} %bitcast.53), custom_call_target="tpu_custom_call" | custom-call | tf_op jit(solution)/shard_map/finish/pallas_call | solution.py:391
  207.3 0.0 copy-done.1
  (9 shorter events, 0.1 us)
Async XLA Ops:
  0.0 85.0 %copy-start = (bf16[576,576]{1,0:T(8,128)(2,1)S(1)}, bf16[576,576]{1,0:T(8,128)(2,1)}, u32[]{:S(2)}) copy-start(bf16[576,576]{1,0:T(8,128)(2,1)} %param.10) | copy-start | bytes 1990660
  57.7 5.8 %copy-start.9 = (bf16[72,5408]{1,0:T(8,128)(2,1)S(1)}, bf16[72,5408]{1,0:T(8,128)(2,1)}, u32[]{:S(2)}) copy-start(bf16[72,5408]{1,0:T(8,128)(2,1)} %param.8) | copy-start | bytes 2336260
  68.6 7.7 %copy-start.6 = (bf16[72,5408]{1,0:T(8,128)(2,1)}, bf16[72,5408]{1,0:T(8,128)(2,1)S(1)}, u32[]{:S(2)}) copy-start(bf16[72,5408]{1,0:T(8,128)(2,1)S(1)} %reshape.52.vo_ref) | copy-start | bytes 2336260
  68.6 2.4 %copy-start.4 = (bf16[8,1,72,1352]{3,2,1,0:T(8,128)(2,1)S(1)}, bf16[8,1,72,1352]{3,2,1,0:T(8,128)(2,1)}, u32[]{:S(2)}) copy-start(bf16[8,1,72,1352]{3,2,1,0:T(8,128)(2,1)} %get-tuple-element.19) | copy-start | bytes 4672516
  74.1 2.2 %copy-start.3 = (bf16[8,1,72,1352]{3,2,1,0:T(8,128)(2,1)S(1)}, bf16[8,1,72,1352]{3,2,1,0:T(8,128)(2,1)}, u32[]{:S(2)}) copy-start(bf16[8,1,72,1352]{3,2,1,0:T(8,128)(2,1)} %get-tuple-element.17) | copy-start | bytes 4672516
  77.7 45.1 %collective-permute-start = (f32[72,576]{0,1:T(8,128)}, f32[72,576]{0,1:T(8,128)}, u32[]{:S(2)}, u32[]{:S(2)}) collective-permute-start(f32[72,576]{0,1:T(8,128)} %convolution_add_fusion), channel_id=1, source_target_pairs={{0,8},{8,0},{1,9},{9,1},{2,10},{10,2},{3,11},{11,3},{4,12},{12,4},... | collective-permute-start | bytes 497672 | tf_op jit(solution)/shard_map/ppermute | solution.py:460
  80.2 3.5 %copy-start.10 = (u32[16]{0:T(128)S(1)}, u32[16]{0:T(128)}, u32[]{:S(2)}) copy-start(u32[16]{0:T(128)} %constant.68) | copy-start | bytes 196
  87.3 1.1 copy-start.8
  93.6 12.6 %slice-start = ((s8[6389760]{0:T(1024)(128)(4,1)}), s8[2195456]{0:T(1024)(128)(4,1)S(1)}, s32[]{:S(2)}) async-start(s8[6389760]{0:T(1024)(128)(4,1)} %bitcast.51), calls=%async_computation | async-start | bytes 4390912
  98.9 4.5 %copy-start.7 = (bf16[8,72,1352]{2,1,0:T(8,128)(2,1)S(1)}, bf16[8,72,1352]{2,1,0:T(8,128)(2,1)}, u32[]{:S(2)}) copy-start(bf16[8,72,1352]{2,1,0:T(8,128)(2,1)} %get-tuple-element.12) | copy-start | bytes 4672516
  98.9 7.4 %slice-start.1 = ((s8[6389760]{0:T(1024)(128)(4,1)}), s8[4194304]{0:T(1024)(128)(4,1)S(1)}, s32[]{:S(2)}) async-start(s8[6389760]{0:T(1024)(128)(4,1)} %bitcast.51), calls=%async_computation.1 | async-start | bytes 8388608
  103.4 2.9 %copy-start.5 = (bf16[3,52,2496]{2,1,0:T(8,128)(2,1)S(1)}, bf16[3,52,2496]{2,1,0:T(8,128)(2,1)}, u32[]{:S(2)}) copy-start(bf16[3,52,2496]{2,1,0:T(8,128)(2,1)} %dot_general.26) | copy-start | bytes 2336260
  107.8 1.8 copy-start.2
  195.6 11.7 %copy-start.1 = (bf16[576,576]{1,0:T(8,128)(2,1)S(1)}, bf16[576,576]{1,0:T(8,128)(2,1)}, u32[]{:S(2)}) copy-start(bf16[576,576]{1,0:T(8,128)(2,1)} %param.10) | copy-start | bytes 1990660
